TPU v7x, 32 devices: a whole 2x2x4 slice. The times are simulated.
32 devices in a mesh: dp: 4 (over y, core), vocab: 8 (over z, x).
Axes of the slice: x: 2, y: 2, z: 4, core: 2. Of those that a mesh axis runs over, the one named last changes fastest.
Arguments:
- hidden: bfloat16 [768, 8192], P('dp', 'vocab'), may hold values from -100 to 100
- proj: bfloat16 [8192, 65536], P(None, ('dp', 'vocab')), may hold values from -3 to 3
- target_ids: int32 [768], replicated, may hold values from 0 to 65535
- seq_len: int32 [16], replicated, may hold values from 1 to 189, as said below
- seq_way: int32 [16], replicated, may hold values from 0 to 3
Outputs:
- token_logprob: float32 [768], P('dp')
- token_entropy: float32 [768], P('dp')
- seq_logprob: float32 [16], replicated
Inputs may be any that keep to these rules, and one draw needn't show every extreme that they name: `seq_len`: each data way is given exactly 4 sequences, which fill its first slots one after another in increasing sequence number; the lengths on one way add up to at most 192, to exactly 192 on some way, and over all ways to exactly 372. Some sequence has exactly 189 tokens.
All inputs are finite; a program needn't handle non-finite values.
Results may differ from a plain program's by a relative error of at most 0.0003.
Values may be sent and summed in bfloat16 or wider, within the bound.
No kernel may reach another device: no remote copies, remote signals or barrier semaphores. Data moves between devices by JAX's collectives and lax.ppermute only.
A program may use at most 128 MiB of HBM per device.

v0:
```python
import jax
import jax.numpy as jnp
from jax import lax
from jax.sharding import PartitionSpec as P


def membership(seq_len, seq_way, slots, ways):
    count = seq_len.shape[0]
    order = jnp.arange(count, dtype=jnp.int32)
    earlier = (seq_way[:, None] == seq_way[None, :]) & (order[:, None] < order[None, :])
    start = jnp.sum(jnp.where(earlier, seq_len[:, None], 0), axis=0)
    row = jnp.arange(slots * ways, dtype=jnp.int32)
    owner = row // slots
    within = row % slots
    return (
        (seq_way[None, :] == owner[:, None])
        & (within[:, None] >= start[None, :])
        & (within[:, None] < (start + seq_len)[None, :])
    )


def target_logit(logits, first_col, targets):
    columns = first_col + jnp.arange(logits.shape[1], dtype=jnp.int32)
    return jnp.sum(jnp.where(targets[:, None] == columns[None, :], logits, 0.0), axis=1)


def per_device(hidden, proj, target_ids, seq_len, seq_way):
    ways = lax.axis_size("dp")
    slots = hidden.shape[0]
    width = proj.shape[1]
    first_col = (lax.axis_index("dp") * lax.axis_size("vocab") + lax.axis_index("vocab")) * width
    member = membership(seq_len, seq_way, slots, ways)
    valid = jnp.any(member, axis=1)
    kept = slots + (ways - 1) * (5 * slots // 16)
    source = jnp.nonzero(valid, size=kept)[0].astype(jnp.int32)
    slot_rows = lax.all_gather(hidden, "dp", axis=0, tiled=True)
    slot_rows = jnp.take(slot_rows, source, axis=0)
    empty = jnp.zeros((slot_rows.shape[0], width), jnp.float32)
    piece = lax.all_gather(slot_rows, "vocab", axis=1, tiled=True)
    weights_part = lax.slice_in_dim(proj, 0, piece.shape[1], axis=0)
    logits = empty + jnp.dot(piece, weights_part, preferred_element_type=jnp.float32)
    targets = jnp.take(target_ids, source)
    top = lax.pmax(jnp.max(logits, axis=1), ("dp", "vocab"))
    shifted = logits - top[:, None]
    weight = jnp.exp(shifted)
    partial_total = jnp.sum(weight, axis=1)
    partial_moment = jnp.sum(weight * shifted, axis=1)
    partial_pick = target_logit(logits, first_col, targets)
    total, moment, picked = lax.psum((partial_total, partial_moment, partial_pick), ("dp", "vocab"))
    log_total = jnp.log(total)
    logprob = picked - top - log_total
    entropy = log_total - moment / total
    position = jnp.clip(jnp.cumsum(valid.astype(jnp.int32)) - 1, 0, kept - 1)
    logprob = jnp.take(logprob, position)
    entropy = jnp.take(entropy, position)
    logprob = jnp.where(valid, logprob, 0.0)
    entropy = jnp.where(valid, entropy, 0.0)
    seq_logprob = jnp.dot(member.astype(jnp.float32).T, logprob, precision=lax.Precision.HIGHEST)
    mine = lax.axis_index("dp") * slots
    return (
        lax.dynamic_slice_in_dim(logprob, mine, slots),
        lax.dynamic_slice_in_dim(entropy, mine, slots),
        seq_logprob,
    )


def solution(mesh):
    placed = (P("dp", "vocab"), P(None, ("dp", "vocab")), P(), P(), P())
    return jax.shard_map(
        per_device, mesh=mesh, in_specs=placed, out_specs=(P("dp"), P("dp"), P()), check_vma=False
    )
```

profile of v0, /device:TPU:0, one launch (start us, length us, event | category | flops | bytes accessed | tf_op | source)
XLA Modules:
  0.0 252.8 jit_solution(5199935121972603821)
XLA Ops:
  7.2 0.0 copy-start
  7.2 0.0 all-gather.3.cloned.1.call-start
  7.2 0.7 all-gather.3.cloned.1.call-update
  7.9 0.0 all-gather.5.cloned.1.call-start
  8.0 0.8 select_reduce_fusion.1
  8.8 0.7 add.90
  9.4 0.8 and_reduce_fusion
  10.2 0.3 reduce-window.16
  10.5 0.1 slice.15
  10.6 0.1 slice_reduce_fusion
  10.7 0.1 add_bitcast_fusion
  10.8 5.8 %scatter_custom_fusion = s32[372]{0:T(512)S(1)} fusion(s32[768]{0:T(1024)S(1)} %fusion.17, s32[768]{0:T(1024)S(1)} %ne.69, s32[]{:T(128)} %constant.99.clone.1), kind=kCustom, calls=%fused_computation.60 | custom fusion | flops 768 | bytes 1492 | tf_op jit(solution)/shard_map/scatter-add | solution.py:35
  16.7 0.3 reduce-window.24
  17.0 0.1 slice.17
  17.1 0.6 convert_reduce_fusion
  17.7 0.1 slice_reduce_fusion.1
  17.9 0.1 add_bitcast_fusion.1
  17.9 0.7 compare_select_fusion.2
  18.6 0.0 copy-done
  18.6 1.9 gather_fusion
  20.5 0.7 broadcast_select_fusion.1
  21.2 10.8 %all-gather.3.cloned.1.call-done = bf16[768,1024]{1,0:T(8,128)(2,1)} async-done(((bf16[192,1024]{1,0:T(8,128)(2,1)}), bf16[768,1024]{1,0:T(8,128)(2,1)}) %all-gather.3.cloned.1.call-update) | async-done | bytes 1572880 | tf_op jit(solution)/shard_map/all_gather | solution.py:36
  32.0 4.4 %gather_fusion.1 = bf16[372,1024]{1,0:T(8,128)(2,1)S(1)} fusion(bf16[768,1024]{1,0:T(8,128)(2,1)} %all-gather.3.cloned.1.call-done, s32[1024]{0:T(1024)S(1)} %pad_clamp_fusion.1), kind=kCustom, calls=%fused_computation.3 | custom fusion | bytes 1525200 | tf_op jit(solution)/shard_map/jit(_take)/gather | solution.py:37
  36.4 1.0 broadcast_select_fusion
  37.4 0.0 all-gather.5.cloned.1.call-update
  37.5 0.1 compare_select_fusion.1
  37.6 97.1 %all-gather.5.cloned.1.call-done = bf16[372,8192]{1,0:T(8,128)(2,1)} async-done(((bf16[372,1024]{1,0:T(8,128)(2,1)}), bf16[372,8192]{1,0:T(8,128)(2,1)}) %all-gather.5.cloned.1.call-update) | async-done | bytes 6094864 | tf_op jit(solution)/shard_map/all_gather | solution.py:39
  134.7 18.9 %fusion.21 = (f32[372]{0:T(512)S(1)}, f32[372,2048]{1,0:T(8,128)S(1)}) fusion(bf16[372,8192]{1,0:T(8,128)(2,1)} %all-gather.5.cloned.1.call-done, bf16[8192,2048]{1,0:T(8,128)(2,1)} %param.8), kind=kOutput, calls=%fused_computation.62 | convolution fusion | flops 12483010560 | bytes 42698192 | tf_op jit(solution)/shard_map/dot_general | solution.py:41
  153.6 38.4 %pmax.7 = f32[372]{0:T(512)S(1)} all-reduce(f32[372]{0:T(512)S(1)} %get-tuple-element.16), channel_id=1, replica_groups=mesh['dp'=4,'vocab'=8] {'dp','vocab'}, use_global_device_ids=true, to_apply=%region_11.12 | all-reduce | flops 372 | bytes 2976 | tf_op jit(solution)/shard_map/pmax | solution.py:43
  192.0 1.1 fusion
  193.1 40.8 %all-reduce.1 = (f32[372]{0:T(512)S(1)}, f32[372]{0:T(512)S(1)}, f32[372]{0:T(512)S(1)}) all-reduce(f32[372]{0:T(512)S(1)} %get-tuple-element.6, f32[372]{0:T(512)S(1)} %get-tuple-element.5, f32[372]{0:T(512)S(1)} %get-tuple-element.4), channel_id=1, replica_groups=mesh['dp'=4,'vocab'=8] {'dp','vocab'}, use_global_device_ids=true, to_apply=%region_9.10 | all-reduce | flops 1116 | bytes 8928 | tf_op jit(solution)/shard_map/psum | solution.py:49
  233.9 5.0 %gather_fusion.2 = f32[768]{0:T(1024)S(1)} fusion(f32[372]{0:T(512)S(1)} %get-tuple-element.14, s32[1024]{0:T(1024)S(1)} %pad_clamp_fusion), kind=kCustom, calls=%fused_computation.clone | custom fusion | bytes 9216 | tf_op jit(solution)/shard_map/jit(_take)/gather | solution.py:54
  238.9 0.0 copy-start.1
  238.9 5.0 %gather_fusion.3 = f32[768]{0:T(1024)S(1)} fusion(f32[372]{0:T(512)S(1)} %get-tuple-element.15, s32[1024]{0:T(1024)S(1)} %pad_clamp_fusion), kind=kCustom, calls=%fused_computation.1.clone | custom fusion | bytes 9216 | tf_op jit(solution)/shard_map/jit(_take)/gather | solution.py:55
  244.0 0.0 copy-done.1
  244.0 0.7 convolution_bitcast_fusion
  244.7 0.6 dynamic_slice.6
  245.4 0.6 dynamic_slice.7
  (14 shorter events, 0.1 us)
Async XLA Ops:
  7.2 11.5 %copy-start = (s32[768]{0:T(1024)S(1)}, s32[768]{0:T(1024)}, u32[]{:S(2)}) copy-start(s32[768]{0:T(1024)} %param.9) | copy-start | bytes 9220
  7.2 24.8 %all-gather.3.cloned.1.call-start = ((), (), s32[]{:S(2)}) async-start(), calls=%async_computation | async-start | bytes 1966080 | tf_op jit(solution)/shard_map/all_gather | solution.py:36
  7.9 126.8 %all-gather.5.cloned.1.call-start = ((), (), s32[]{:S(2)}) async-start(), calls=%async_computation.1 | async-start | bytes 6930432 | tf_op jit(solution)/shard_map/all_gather | solution.py:39
  238.9 5.1 %copy-start.1 = (s32[16]{0:T(128)S(1)}, s32[16]{0:T(128)}, u32[]{:S(2)}) copy-start(s32[16]{0:T(128)} %param.11) | copy-start | bytes 196
Sparse Core Ops, SparseCore 0:
  9.5 22.3 all-gather.2
  37.6 97.0 all-gather.4
where the time goes:
time: 253 us
  waiting for transfers between devices  109 us (43%)
  blocking collectives  79.2 us (31%)
  matrix products  19.6 us (8%)
  local copies, waits for them, and re-layouts  18 us (7%)
  between operations  14.2 us (6%)
  other arithmetic  13.1 us (5%)
    all_gather x1, waiting for transfers between devices, per_device(): piece = lax.all_gather(slot_rows, 'vocab', axis=1, tiled=True)  97.1 us
    psum x1, blocking collectives, per_device(): lax.psum((partial_total, partial_moment, partial_pick), ('dp', 'vocab'))  40.8 us
    pmax x1, blocking collectives, per_device(): top = lax.pmax(jnp.max(logits, axis=1), ('dp', 'vocab'))  38.4 us
    dot_general x1, matrix products, per_device(): jnp.dot(piece, weights_part, preferred_element_type=jnp.float32)  18.9 us
    all_gather x1, waiting for transfers between devices, per_device(): slot_rows = lax.all_gather(hidden, 'dp', axis=0, tiled=True)  10.8 us
    scatter-add x1, other arithmetic, per_device(): source = jnp.nonzero(valid, size=kept)[0].astype(jnp.int32)  5.85 us
  transfers between devices with their start and end apart: 2, of which 2 were waited for; matrix products, arithmetic and copies ran while one was open for 5% of the time, Pallas kernels for 0%

commit v1 on v0

--- a/solution.py
+++ b/solution.py
@@ -46,7 +46,9 @@
     partial_total = jnp.sum(weight, axis=1)
     partial_moment = jnp.sum(weight * shifted, axis=1)
     partial_pick = target_logit(logits, first_col, targets)
-    total, moment, picked = lax.psum((partial_total, partial_moment, partial_pick), ("dp", "vocab"))
+    total, moment, picked = lax.psum(
+        lax.psum((partial_total, partial_moment, partial_pick), "vocab"), "dp"
+    )
     log_total = jnp.log(total)
     logprob = picked - top - log_total
     entropy = log_total - moment / total

time: 253 us -> 240 us (0.949)
  blocking collectives: 79.2 us -> 65.5 us
    psum x1 -> x2, blocking collectives: 40.8 us -> 27.1 us  [the longest x1 21.3 us: per_device(): lax.psum((partial_total, partial_moment, partial_pick), 'vocab')]
  transfers between devices with their start and end apart: 2 -> 2, of which waited for: 2 -> 2; matrix products, arithmetic and copies ran while one was open for 5% -> 6% of each run, Pallas kernels for 0% -> 0%
where the time goes in v1:
time: 240 us; the launch traced here: 239 us
  waiting for transfers between devices  109 us (45%)
  blocking collectives  65.5 us (27%)
  matrix products  19.6 us (8%)
  local copies, waits for them, and re-layouts  18 us (8%)
  between operations  14.2 us (6%)
  other arithmetic  13.1 us (5%)
    all_gather x1, waiting for transfers between devices, per_device(): piece = lax.all_gather(slot_rows, 'vocab', axis=1, tiled=True)  97.1 us
    pmax x1, blocking collectives, per_device(): top = lax.pmax(jnp.max(logits, axis=1), ('dp', 'vocab'))  38.4 us
    psum x1, blocking collectives, per_device(): lax.psum((partial_total, partial_moment, partial_pick), 'vocab')  21.3 us
    dot_general x1, matrix products, per_device(): jnp.dot(piece, weights_part, preferred_element_type=jnp.float32)  18.9 us
    all_gather x1, waiting for transfers between devices, per_device(): slot_rows = lax.all_gather(hidden, 'dp', axis=0, tiled=True)  10.8 us
    scatter-add x1, other arithmetic, per_device(): source = jnp.nonzero(valid, size=kept)[0].astype(jnp.int32)  5.85 us
    psum x1, blocking collectives, per_device(): lax.psum(lax.psum((partial_total, partial_moment, partial_pick), 'vocab')...  5.74 us
    gather x1, local copies, waits for them, and re-layouts, per_device(): entropy = jnp.take(entropy, position)  5.01 us
  transfers between devices with their start and end apart: 2, of which 2 were waited for; matrix products, arithmetic and copies ran while one was open for 6% of the time, Pallas kernels for 0%

profile of v1, /device:TPU:0, one launch (start us, length us, event | category | flops | bytes accessed | tf_op | source)
XLA Modules:
  0.0 239.1 jit_solution(5951062352761225107)
XLA Ops:
  7.2 0.0 copy-start
  7.2 0.0 all-gather.3.cloned.1.call-start
  7.2 0.7 all-gather.3.cloned.1.call-update
  7.9 0.0 all-gather.5.cloned.1.call-start
  8.0 0.8 select_reduce_fusion.1
  8.8 0.7 add.96
  9.4 0.8 and_reduce_fusion
  10.2 0.3 reduce-window.16
  10.5 0.1 slice.15
  10.6 0.1 slice_reduce_fusion
  10.7 0.1 add_bitcast_fusion
  10.8 5.8 %scatter_custom_fusion = s32[372]{0:T(512)S(1)} fusion(s32[768]{0:T(1024)S(1)} %fusion.17, s32[768]{0:T(1024)S(1)} %ne.69, s32[]{:T(128)} %constant.99.clone.1), kind=kCustom, calls=%fused_computation.60 | custom fusion | flops 768 | bytes 1492 | tf_op jit(solution)/shard_map/scatter-add | solution.py:35
  16.7 0.3 reduce-window.24
  17.0 0.1 slice.17
  17.1 0.6 convert_reduce_fusion
  17.7 0.1 slice_reduce_fusion.1
  17.9 0.1 add_bitcast_fusion.1
  17.9 0.7 compare_select_fusion.2
  18.6 0.0 copy-done
  18.6 1.9 gather_fusion
  20.5 0.7 broadcast_select_fusion.1
  21.2 10.8 %all-gather.3.cloned.1.call-done = bf16[768,1024]{1,0:T(8,128)(2,1)} async-done(((bf16[192,1024]{1,0:T(8,128)(2,1)}), bf16[768,1024]{1,0:T(8,128)(2,1)}) %all-gather.3.cloned.1.call-update) | async-done | bytes 1572880 | tf_op jit(solution)/shard_map/all_gather | solution.py:36
  32.0 4.4 %gather_fusion.1 = bf16[372,1024]{1,0:T(8,128)(2,1)S(1)} fusion(bf16[768,1024]{1,0:T(8,128)(2,1)} %all-gather.3.cloned.1.call-done, s32[1024]{0:T(1024)S(1)} %pad_clamp_fusion.1), kind=kCustom, calls=%fused_computation.3 | custom fusion | bytes 1525200 | tf_op jit(solution)/shard_map/jit(_take)/gather | solution.py:37
  36.4 1.0 broadcast_select_fusion
  37.4 0.0 all-gather.5.cloned.1.call-update
  37.5 0.1 compare_select_fusion.1
  37.6 97.1 %all-gather.5.cloned.1.call-done = bf16[372,8192]{1,0:T(8,128)(2,1)} async-done(((bf16[372,1024]{1,0:T(8,128)(2,1)}), bf16[372,8192]{1,0:T(8,128)(2,1)}) %all-gather.5.cloned.1.call-update) | async-done | bytes 6094864 | tf_op jit(solution)/shard_map/all_gather | solution.py:39
  134.7 18.9 %fusion.21 = (f32[372]{0:T(512)S(1)}, f32[372,2048]{1,0:T(8,128)S(1)}) fusion(bf16[372,8192]{1,0:T(8,128)(2,1)} %all-gather.5.cloned.1.call-done, bf16[8192,2048]{1,0:T(8,128)(2,1)} %param.8), kind=kOutput, calls=%fused_computation.62 | convolution fusion | flops 12483010560 | bytes 42698192 | tf_op jit(solution)/shard_map/dot_general | solution.py:41
  153.6 38.4 %pmax.7 = f32[372]{0:T(512)S(1)} all-reduce(f32[372]{0:T(512)S(1)} %get-tuple-element.19), channel_id=1, replica_groups=mesh['dp'=4,'vocab'=8] {'dp','vocab'}, use_global_device_ids=true, to_apply=%region_12.13 | all-reduce | flops 372 | bytes 2976 | tf_op jit(solution)/shard_map/pmax | solution.py:43
  192.0 1.1 fusion
  193.1 21.3 %all-reduce.1 = (f32[372]{0:T(512)S(1)}, f32[372]{0:T(512)S(1)}, f32[372]{0:T(512)S(1)}) all-reduce(f32[372]{0:T(512)S(1)} %get-tuple-element.6, f32[372]{0:T(512)S(1)} %get-tuple-element.5, f32[372]{0:T(512)S(1)} %get-tuple-element.4), channel_id=1, replica_groups=mesh['dp'=4,'vocab'=8] {'vocab'}, use_global_device_ids=true, to_apply=%region_9.10 | all-reduce | flops 1116 | bytes 8928 | tf_op jit(solution)/shard_map/psum | solution.py:50
  214.4 5.7 %all-reduce.2 = (f32[372]{0:T(512)S(1)}, f32[372]{0:T(512)S(1)}, f32[372]{0:T(512)S(1)}) all-reduce(f32[372]{0:T(512)S(1)} %get-tuple-element.7, f32[372]{0:T(512)S(1)} %get-tuple-element.8, f32[372]{0:T(512)S(1)} %get-tuple-element.9), channel_id=1, replica_groups=mesh['dp'=4,'vocab'=8] {'dp'}, use_global_device_ids=true, to_apply=%region_10.11 | all-reduce | flops 1116 | bytes 8928 | tf_op jit(solution)/shard_map/psum | solution.py:49
  220.2 5.0 %gather_fusion.2 = f32[768]{0:T(1024)S(1)} fusion(f32[372]{0:T(512)S(1)} %get-tuple-element.17, s32[1024]{0:T(1024)S(1)} %pad_clamp_fusion), kind=kCustom, calls=%fused_computation.clone | custom fusion | bytes 9216 | tf_op jit(solution)/shard_map/jit(_take)/gather | solution.py:56
  225.2 0.0 copy-start.1
  225.2 5.0 %gather_fusion.3 = f32[768]{0:T(1024)S(1)} fusion(f32[372]{0:T(512)S(1)} %get-tuple-element.18, s32[1024]{0:T(1024)S(1)} %pad_clamp_fusion), kind=kCustom, calls=%fused_computation.1.clone | custom fusion | bytes 9216 | tf_op jit(solution)/shard_map/jit(_take)/gather | solution.py:57
  230.3 0.0 copy-done.1
  230.3 0.7 convolution_bitcast_fusion
  231.0 0.6 dynamic_slice.6
  231.7 0.6 dynamic_slice.7
  (14 shorter events, 0.1 us)
Async XLA Ops:
  7.2 11.5 %copy-start = (s32[768]{0:T(1024)S(1)}, s32[768]{0:T(1024)}, u32[]{:S(2)}) copy-start(s32[768]{0:T(1024)} %param.9) | copy-start | bytes 9220
  7.2 24.8 %all-gather.3.cloned.1.call-start = ((), (), s32[]{:S(2)}) async-start(), calls=%async_computation | async-start | bytes 1966080 | tf_op jit(solution)/shard_map/all_gather | solution.py:36
  7.9 126.8 %all-gather.5.cloned.1.call-start = ((), (), s32[]{:S(2)}) async-start(), calls=%async_computation.1 | async-start | bytes 6930432 | tf_op jit(solution)/shard_map/all_gather | solution.py:39
  225.2 5.1 %copy-start.1 = (s32[16]{0:T(128)S(1)}, s32[16]{0:T(128)}, u32[]{:S(2)}) copy-start(s32[16]{0:T(128)} %param.11) | copy-start | bytes 196
Sparse Core Ops, SparseCore 0:
  9.5 22.3 all-gather.2
  37.6 97.0 all-gather.4
